TPU v7x, 32 devices: a whole 2x2x4 slice. The times are simulated.
32 devices in a mesh: row: 4 (over x, core), col: 8 (over z, y).
Axes of the slice: x: 2, y: 2, z: 4, core: 2. Of those that a mesh axis runs over, the one named last changes fastest.
Arguments:
- dosage: bfloat16 [1536, 24576], P(None, ('row', 'col')), may hold values from 0 to 2
- zscores: bfloat16 [24576], P(('row', 'col')), may hold values from -18 to 18
- band_reach: int32 [32], replicated, may hold values from 0 to 2, as said below
Outputs:
- ld_tiles: bfloat16 [24576, 3840], P(('row', 'col'))
- smoothed: float32 [24576], P(('row', 'col'))
- quadratic: float32 [], replicated
Inputs may be any that keep to these rules, and one draw needn't show every extreme that they name: `band_reach`: the first 3 blocks, the last 3 blocks and some two neighbouring blocks reach 2.
All inputs are finite; a program needn't handle non-finite values.
Results may differ from a plain program's by a relative error of at most 0.0042.
Values may be sent and summed in bfloat16 or wider, within the bound.
A program may use at most 64 MiB of HBM per device.

v0:
```python
import jax
import jax.numpy as jnp
from jax import lax
from jax.sharding import PartitionSpec as P

BAND = 2


def passed_along(value, axis, steps):
    count = lax.axis_size(axis)
    initial, last = (max(0, -steps), min(count, count - steps))
    return lax.ppermute(value, axis, [(source, source + steps) for source in range(initial, last)])


def standardize(dosage):
    values = dosage.astype(jnp.float32)
    column_mean = jnp.mean(values, axis=0)
    centered = values - column_mean
    variance = jnp.mean(centered * centered, axis=0)
    return (centered * lax.rsqrt(variance + 1e-05)).astype(jnp.bfloat16)


def body(dosage, zscores, band_reach):
    samples = dosage.shape[0]
    block_width = zscores.shape[0]
    block_count = lax.axis_size(("row", "col"))
    position = lax.axis_index(("row", "col"))
    scaled = standardize(dosage)
    own_reach = lax.dynamic_index_in_dim(band_reach, position, 0, False)

    def allowed(offset):
        other = position + offset
        inside = (other >= 0) & (other < block_count)
        their_reach = lax.dynamic_index_in_dim(
            band_reach, jnp.clip(other, 0, block_count - 1), 0, False
        )
        return inside & (abs(offset) <= jnp.minimum(own_reach, their_reach))

    def make_tile(left, right, offset):
        product = (
            lax.dot_general(
                left, right, (((0,), (0,)), ((), ())), preferred_element_type=jnp.float32
            )
            / samples
        )
        return jnp.where(allowed(offset), product, 0.0).astype(jnp.bfloat16)

    def apply_tile(ld_tile, near_scores):
        return jnp.dot(ld_tile, near_scores, preferred_element_type=jnp.float32)

    own_z = zscores.astype(jnp.float32)
    tile_map = {0: make_tile(scaled, scaled, 0)}
    score_map = {0: zscores}
    for offset in range(1, BAND + 1):
        far_scaled, far_z = passed_along((scaled, zscores), ("row", "col"), -offset)
        tile_map[offset] = make_tile(scaled, far_scaled, offset)
        score_map[offset] = far_z
    terms = {}
    for offset in range(0, BAND + 1):
        terms[offset] = apply_tile(tile_map[offset], score_map[offset])
    total = None
    for offset in range(1, BAND + 1):
        returned, returned_z = passed_along((tile_map[offset], zscores), ("row", "col"), offset)
        tile_map[-offset] = returned.T
        score_map[-offset] = returned_z
    for offset in range(1, BAND + 1):
        terms[-offset] = apply_tile(tile_map[-offset], score_map[-offset])
    smoothed = terms[0]
    for offset in range(1, BAND + 1):
        smoothed = smoothed + terms[offset] + terms[-offset]
    total = lax.psum(jnp.sum(own_z * smoothed), ("row", "col"))
    quadratic = total / (block_count * block_width)
    ld_tiles = jnp.concatenate([tile_map[offset] for offset in range(-BAND, BAND + 1)], axis=1)
    return (ld_tiles, smoothed, quadratic)


def solution(mesh):
    placed = (P(None, ("row", "col")), P(("row", "col")), P())
    return jax.shard_map(
        body,
        mesh=mesh,
        in_specs=placed,
        out_specs=(P(("row", "col"), None), P(("row", "col")), P()),
        check_vma=False,
    )
```

profile of v0, /device:TPU:9, one launch (start us, length us, event | category | flops | bytes accessed | tf_op | source)
XLA Modules:
  0.0 223.7 jit_solution(9568745591780098309)
XLA Ops:
  0.6 0.0 copy-start
  0.6 2.2 convert_reduce_fusion
  2.9 0.1 copy-done
  3.0 0.7 fusion.2
  3.7 2.0 fusion.3
  5.7 3.0 %collective-permute-start.2 = (bf16[1536,768]{1,0:T(8,128)(2,1)}, bf16[1536,768]{1,0:T(8,128)(2,1)}, u32[]{:S(2)}, u32[]{:S(2)}) collective-permute-start(bf16[1536,768]{1,0:T(8,128)(2,1)} %fusion.3), channel_id=1, source_target_pairs={{1,0},{2,1},{3,2},{4,3},{5,4},{6,5},{7,6},{8,7},{9,8},{10,9},{11,1... | collective-permute-start | bytes 7077896 | tf_op jit(solution)/shard_map/ppermute | solution.py:12
  8.7 5.8 %collective-permute-start = (bf16[1536,768]{1,0:T(8,128)(2,1)}, bf16[1536,768]{1,0:T(8,128)(2,1)}, u32[]{:S(2)}, u32[]{:S(2)}) collective-permute-start(bf16[1536,768]{1,0:T(8,128)(2,1)} %fusion.3), channel_id=1, source_target_pairs={{2,0},{3,1},{4,2},{5,3},{6,4},{7,5},{8,6},{9,7},{10,8},{11,9},{12,... | collective-permute-start | bytes 7077896 | tf_op jit(solution)/shard_map/ppermute | solution.py:12
  14.5 0.0 copy-done.4
  14.6 0.7 fusion.10
  17.6 42.4 %collective-permute-done.2 = bf16[1536,768]{1,0:T(8,128)(2,1)} collective-permute-done((bf16[1536,768]{1,0:T(8,128)(2,1)}, bf16[1536,768]{1,0:T(8,128)(2,1)}, u32[]{:S(2)}, u32[]{:S(2)}) %collective-permute-start.2) | collective-permute-done | bytes 2359328 | tf_op jit(solution)/shard_map/ppermute | solution.py:12
  60.0 4.4 %select_convert_fusion.1 = bf16[768,768]{0,1:T(8,128)(2,1)S(1)} fusion(bf16[1536,768]{1,0:T(8,128)(2,1)} %fusion.3, bf16[1536,768]{1,0:T(8,128)(2,1)} %collective-permute-done.2, pred[]{:T(512)S(6)} %and.23), kind=kOutput, calls=%fused_computation.7 | convolution fusion | flops 1813708800 | bytes 5898241 | tf_op jit(solution)/shard_map/dot_general | solution.py:41
  64.5 4.0 %collective-permute-start.3 = (bf16[768,768]{0,1:T(8,128)(2,1)S(1)}, bf16[768,768]{0,1:T(8,128)(2,1)S(1)}, u32[]{:S(2)}, u32[]{:S(2)}) collective-permute-start(bf16[768,768]{0,1:T(8,128)(2,1)S(1)} %select_convert_fusion.1), channel_id=1, source_target_pairs={{0,1},{1,2},{2,3},{3,4},{4,5},{5,6},{6,7},{7,8},{8,9},{9,10},{10,1... | collective-permute-start | bytes 3538952 | tf_op jit(solution)/shard_map/ppermute | solution.py:12
  68.5 43.0 %collective-permute-done = bf16[1536,768]{1,0:T(8,128)(2,1)} collective-permute-done((bf16[1536,768]{1,0:T(8,128)(2,1)}, bf16[1536,768]{1,0:T(8,128)(2,1)}, u32[]{:S(2)}, u32[]{:S(2)}) %collective-permute-start) | collective-permute-done | bytes 2359328 | tf_op jit(solution)/shard_map/ppermute | solution.py:12
  111.5 4.4 %select_convert_fusion.2 = bf16[768,768]{0,1:T(8,128)(2,1)S(1)} fusion(bf16[1536,768]{1,0:T(8,128)(2,1)} %fusion.3, bf16[1536,768]{1,0:T(8,128)(2,1)} %collective-permute-done, pred[]{:T(512)S(6)} %and.21), kind=kOutput, calls=%fused_computation.8 | convolution fusion | flops 1813708800 | bytes 5898241 | tf_op jit(solution)/shard_map/dot_general | solution.py:41
  116.0 0.0 copy-start.5
  116.0 1.4 copy.6
  117.4 3.2 %collective-permute-start.1 = (bf16[768,768]{1,0:T(8,128)(2,1)}, bf16[768,768]{1,0:T(8,128)(2,1)}, u32[]{:S(2)}, u32[]{:S(2)}) collective-permute-start(bf16[768,768]{1,0:T(8,128)(2,1)} %copy.6), channel_id=1, source_target_pairs={{0,2},{1,3},{2,4},{3,5},{4,6},{5,7},{6,8},{7,9},{8,10},{9,11},{10,... | collective-permute-start | bytes 3538952 | tf_op jit(solution)/shard_map/ppermute | solution.py:12
  120.6 0.0 copy-done.5
  120.6 2.1 collective-permute-start.6
  122.7 1.9 collective-permute-start.5
  124.7 4.3 %collective-permute-start.4 = (bf16[768]{0:T(1024)(128)(2,1)S(1)}, bf16[768]{0:T(1024)(128)(2,1)}, u32[]{:S(2)}, u32[]{:S(2)}) collective-permute-start(bf16[768]{0:T(1024)(128)(2,1)S(1)} %copy-done.5), channel_id=1, source_target_pairs={{1,0},{2,1},{3,2},{4,3},{5,4},{6,5},{7,6},{8,7},{9,8},{10,9},{11,1... | collective-permute-start | bytes 4616 | tf_op jit(solution)/shard_map/ppermute | solution.py:12
  128.9 2.6 %collective-permute-done.6 = bf16[768]{0:T(1024)(128)(2,1)S(1)} collective-permute-done((bf16[768]{0:T(1024)(128)(2,1)S(1)}, bf16[768]{0:T(1024)(128)(2,1)S(1)}, u32[]{:S(2)}, u32[]{:S(2)}) %collective-permute-start.6) | collective-permute-done | bytes 1568 | tf_op jit(solution)/shard_map/ppermute | solution.py:12
  131.5 19.6 %collective-permute-start.7 = (bf16[768]{0:T(1024)(128)(2,1)S(1)}, bf16[768]{0:T(1024)(128)(2,1)}, u32[]{:S(2)}, u32[]{:S(2)}) collective-permute-start(bf16[768]{0:T(1024)(128)(2,1)S(1)} %copy-done.5), channel_id=1, source_target_pairs={{0,2},{1,3},{2,4},{3,5},{4,6},{5,7},{6,8},{7,9},{8,10},{9,11},{10,... | collective-permute-start | bytes 4616 | tf_op jit(solution)/shard_map/ppermute | solution.py:12
  152.3 0.0 collective-permute-done.5
  152.3 0.0 collective-permute-done.4
  152.3 0.7 reshape.25
  153.0 0.0 collective-permute-done.7
  153.0 1.2 reshape.31
  154.3 0.3 convolution_reduce_fusion.2
  154.5 0.3 convolution_reduce_fusion
  154.8 0.0 collective-permute-done.3
  154.8 1.5 copy.7
  156.3 0.0 collective-permute-done.1
  156.3 2.5 %bitcast_dynamic-update-slice_fusion = bf16[768,3840]{0,1:T(8,128)(2,1)} fusion(bf16[768,768]{1,0:T(8,128)(2,1)} %collective-permute-done.1), kind=kLoop, calls=%fused_computation.11 | loop fusion | bytes 2359296
  158.8 0.0 copy-done.1
  158.8 1.1 constant_dynamic-update-slice_fusion.3
  159.9 5.8 %constant_dynamic-update-slice_fusion.2 = (bf16[768,3840]{0,1:T(8,128)(2,1)}, bf16[768,768]{0,1:T(8,128)(2,1)}) fusion(bf16[768,3840]{0,1:T(8,128)(2,1)} %constant_dynamic-update-slice_fusion.3, bf16[1536,768]{1,0:T(8,128)(2,1)} %fusion.3, pred[]{:T(512)S(6)} %and.25), kind=kOutput, calls=%fused_computation.19 | convolution fusion | flops 1813708800 | bytes 7077889 | tf_op jit(solution)/shard_map/dot_general | solution.py:41
  165.7 1.1 constant_dynamic-update-slice_fusion.1
  166.8 1.1 constant_dynamic-update-slice_fusion
  167.9 8.5 %copy.8 = bf16[768,3840]{1,0:T(8,128)(2,1)} copy(bf16[768,3840]{0,1:T(8,128)(2,1)} %constant_dynamic-update-slice_fusion) | data formatting | bytes 11796480
  176.4 0.0 copy-done.2
  176.4 0.3 convolution_reduce_fusion.3
  176.7 0.4 convolution_reduce_fusion.1
  177.2 0.0 copy-done.3
  177.2 1.6 fusion.6
  178.7 0.0 copy-done.6
  178.7 1.2 multiply_reduce_fusion
  179.9 42.0 %psum.7 = f32[]{:T(128)} all-reduce(f32[]{:T(128)} %get-tuple-element.6), channel_id=1, replica_groups=mesh['row'=4,'col'=8] {'row','col'}, use_global_device_ids=true, to_apply=%region_3.4 | all-reduce | flops 1 | bytes 8 | tf_op jit(solution)/shard_map/psum | solution.py:71
  (10 shorter events, 0.0 us)
Async XLA Ops:
  0.6 2.4 %copy-start = (bf16[1536,768]{1,0:T(8,128)(2,1)S(1)}, bf16[1536,768]{1,0:T(8,128)(2,1)}, u32[]{:S(2)}) copy-start(bf16[1536,768]{1,0:T(8,128)(2,1)} %param.3) | copy-start | bytes 7077892
  3.7 10.9 %copy-start.4 = (s32[32]{0:T(128)S(1)}, s32[32]{0:T(128)}, u32[]{:S(2)}) copy-start(s32[32]{0:T(128)} %param.5) | copy-start | bytes 388
  5.7 54.3 %collective-permute-start.2 = (bf16[1536,768]{1,0:T(8,128)(2,1)}, bf16[1536,768]{1,0:T(8,128)(2,1)}, u32[]{:S(2)}, u32[]{:S(2)}) collective-permute-start(bf16[1536,768]{1,0:T(8,128)(2,1)} %fusion.3), channel_id=1, source_target_pairs={{1,0},{2,1},{3,2},{4,3},{5,4},{6,5},{7,6},{8,7},{9,8},{10,9},{11,1... | collective-permute-start | bytes 7077896 | tf_op jit(solution)/shard_map/ppermute | solution.py:12
  8.7 102.8 %collective-permute-start = (bf16[1536,768]{1,0:T(8,128)(2,1)}, bf16[1536,768]{1,0:T(8,128)(2,1)}, u32[]{:S(2)}, u32[]{:S(2)}) collective-permute-start(bf16[1536,768]{1,0:T(8,128)(2,1)} %fusion.3), channel_id=1, source_target_pairs={{2,0},{3,1},{4,2},{5,3},{6,4},{7,5},{8,6},{9,7},{10,8},{11,9},{12,... | collective-permute-start | bytes 7077896 | tf_op jit(solution)/shard_map/ppermute | solution.py:12
  64.5 90.4 %collective-permute-start.3 = (bf16[768,768]{0,1:T(8,128)(2,1)S(1)}, bf16[768,768]{0,1:T(8,128)(2,1)S(1)}, u32[]{:S(2)}, u32[]{:S(2)}) collective-permute-start(bf16[768,768]{0,1:T(8,128)(2,1)S(1)} %select_convert_fusion.1), channel_id=1, source_target_pairs={{0,1},{1,2},{2,3},{3,4},{4,5},{5,6},{6,7},{7,8},{8,9},{9,10},{10,1... | collective-permute-start | bytes 3538952 | tf_op jit(solution)/shard_map/ppermute | solution.py:12
  116.0 4.7 %copy-start.5 = (bf16[768]{0:T(1024)(128)(2,1)S(1)}, bf16[768]{0:T(1024)(128)(2,1)}, u32[]{:S(2)}) copy-start(bf16[768]{0:T(1024)(128)(2,1)} %param.4) | copy-start | bytes 4612
  117.4 38.9 %collective-permute-start.1 = (bf16[768,768]{1,0:T(8,128)(2,1)}, bf16[768,768]{1,0:T(8,128)(2,1)}, u32[]{:S(2)}, u32[]{:S(2)}) collective-permute-start(bf16[768,768]{1,0:T(8,128)(2,1)} %copy.6), channel_id=1, source_target_pairs={{0,2},{1,3},{2,4},{3,5},{4,6},{5,7},{6,8},{7,9},{8,10},{9,11},{10,... | collective-permute-start | bytes 3538952 | tf_op jit(solution)/shard_map/ppermute | solution.py:12
  120.6 10.8 %collective-permute-start.6 = (bf16[768]{0:T(1024)(128)(2,1)S(1)}, bf16[768]{0:T(1024)(128)(2,1)S(1)}, u32[]{:S(2)}, u32[]{:S(2)}) collective-permute-start(bf16[768]{0:T(1024)(128)(2,1)S(1)} %copy-done.5), channel_id=1, source_target_pairs={{2,0},{3,1},{4,2},{5,3},{6,4},{7,5},{8,6},{9,7},{10,8},{11,9},{12,... | collective-permute-start | bytes 4616 | tf_op jit(solution)/shard_map/ppermute | solution.py:12
  122.7 29.6 %collective-permute-start.5 = (bf16[768]{0:T(1024)(128)(2,1)S(1)}, bf16[768]{0:T(1024)(128)(2,1)S(1)}, u32[]{:S(2)}, u32[]{:S(2)}) collective-permute-start(bf16[768]{0:T(1024)(128)(2,1)S(1)} %copy-done.5), channel_id=1, source_target_pairs={{0,1},{1,2},{2,3},{3,4},{4,5},{5,6},{6,7},{7,8},{8,9},{9,10},{10,1... | collective-permute-start | bytes 4616 | tf_op jit(solution)/shard_map/ppermute | solution.py:12
  124.7 27.7 %collective-permute-start.4 = (bf16[768]{0:T(1024)(128)(2,1)S(1)}, bf16[768]{0:T(1024)(128)(2,1)}, u32[]{:S(2)}, u32[]{:S(2)}) collective-permute-start(bf16[768]{0:T(1024)(128)(2,1)S(1)} %copy-done.5), channel_id=1, source_target_pairs={{1,0},{2,1},{3,2},{4,3},{5,4},{6,5},{7,6},{8,7},{9,8},{10,9},{11,1... | collective-permute-start | bytes 4616 | tf_op jit(solution)/shard_map/ppermute | solution.py:12
  131.5 21.5 %collective-permute-start.7 = (bf16[768]{0:T(1024)(128)(2,1)S(1)}, bf16[768]{0:T(1024)(128)(2,1)}, u32[]{:S(2)}, u32[]{:S(2)}) collective-permute-start(bf16[768]{0:T(1024)(128)(2,1)S(1)} %copy-done.5), channel_id=1, source_target_pairs={{0,2},{1,3},{2,4},{3,5},{4,6},{5,7},{6,8},{7,9},{8,10},{9,11},{10,... | collective-permute-start | bytes 4616 | tf_op jit(solution)/shard_map/ppermute | solution.py:12
  156.3 2.5 %copy-start.1 = (bf16[768,768]{0,1:T(8,128)(2,1)S(1)}, bf16[768,768]{0,1:T(8,128)(2,1)}, u32[]{:S(2)}) copy-start(bf16[768,768]{0,1:T(8,128)(2,1)} %copy.7) | copy-start | bytes 3538948
  167.9 8.5 %copy-start.2 = (bf16[768,768]{0,1:T(8,128)(2,1)S(1)}, bf16[768,768]{0,1:T(8,128)(2,1)}, u32[]{:S(2)}) copy-start(bf16[768,768]{0,1:T(8,128)(2,1)} %get-tuple-element.13) | copy-start | bytes 3538948
  176.4 0.8 copy-start.3
  176.4 2.3 %copy-start.6 = (bf16[768]{0:T(1024)(128)(2,1)S(1)}, bf16[768]{0:T(1024)(128)(2,1)}, u32[]{:S(2)}) copy-start(bf16[768]{0:T(1024)(128)(2,1)} %param.4) | copy-start | bytes 4612
where the time goes:
time: 226 us; the launch traced here: 224 us
  waiting for transfers between devices  88 us (39%)
  starting transfers between devices  43.9 us (19%)
  blocking collectives  42 us (19%)
  local copies, waits for them, and re-layouts  19.9 us (9%)
  matrix products  17.5 us (8%)
  between operations  6.25 us (3%)
  other arithmetic  6.11 us (3%)
    ppermute x8, waiting for transfers between devices, passed_along(): lax.ppermute(value, axis, [(source, source + steps) for source in range(i...  88 us
    ppermute x8, starting transfers between devices, passed_along(): lax.ppermute(value, axis, [(source, source + steps) for source in range(i...  43.9 us
    psum x1, blocking collectives, body(): total = lax.psum(jnp.sum(own_z * smoothed), ('row', 'col'))  42 us
    dot_general x3, matrix products, make_tile(): lax.dot_general(left, right, (((0,), (0,)), ((), ())), preferred_element_...  14.7 us
    unnamed x19, local copies, waits for them, and re-layouts  13.3 us
  transfers between devices with their start and end apart: 8, of which 3 were waited for; matrix products, arithmetic and copies ran while one was open for 7% of the time, Pallas kernels for 0%

commit v1 on v0

v1 whole, which is shorter than its diff:
```python
import functools

import jax
import jax.numpy as jnp
from jax import lax
from jax.experimental import pallas as pl
from jax.experimental.pallas import tpu as pltpu
from jax.sharding import PartitionSpec as P

BAND = 2
AXES = ("row", "col")
CHUNKS = 3
ZROWS = 16
MESH = pl.DeviceIdType.MESH


def standardize(chunk):
    values = chunk.astype(jnp.float32)
    column_mean = jnp.mean(values, axis=0, keepdims=True)
    centered = values - column_mean
    variance = jnp.mean(centered * centered, axis=0, keepdims=True)
    return (centered * lax.rsqrt(variance + 1e-05)).astype(jnp.bfloat16)


def kernel(
    rows, cols, flags, dosage, z_in, out, smooth, quad,
    raw, far_raw, part_raw, own, far, part, back_out, side_out, back_in, side_in,
    near_z, col_sums, row_sums, sum_out,
    local_sem, far_send, far_recv, part_send, part_recv, back_send, back_recv,
    side_send, side_recv, z_send, z_recv, col_send, col_recv, row_send, row_recv,
):
    samples, block = dosage.shape
    width = block // CHUNKS
    count = rows * cols
    row, col = lax.axis_index("row"), lax.axis_index("col")
    me = row * cols + col
    sign = 1 - 2 * (me % 2)

    def device(index):
        return (index // cols, index % cols)

    def present(index):
        return (index >= 0) & (index < count)

    onward, source, partner = me - 2 * sign, me + 2 * sign, me + sign
    has_onward, has_source = present(onward), present(source)
    offsets = (-2, -1, 1, 2)

    loads = []
    for k in range(CHUNKS):
        load = pltpu.make_async_copy(
            dosage.at[:, pl.ds(k * width, width)], raw.at[k], local_sem.at[k]
        )
        load.start()
        loads.append(load)
    near_z[...] = jnp.zeros_like(near_z)

    barrier = pltpu.get_barrier_semaphore()
    peers = cols - 1 + rows - 1
    for offset in offsets:
        outside = present(me + offset) & ((me + offset) // cols != row)
        peers = peers + jnp.where(outside, 1, 0)
        @pl.when(outside)
        def _():
            pl.semaphore_signal(
                barrier, inc=1, device_id=device(me + offset), device_id_type=MESH
            )
    for i in range(1, cols):
        pl.semaphore_signal(
            barrier, inc=1, device_id=(row, (col + i) % cols), device_id_type=MESH
        )
    for i in range(1, rows):
        pl.semaphore_signal(
            barrier, inc=1, device_id=((row + i) % rows, col), device_id_type=MESH
        )
    pl.semaphore_wait(barrier, peers)

    def remote(src, dst, send, recv, target):
        return pltpu.make_async_remote_copy(
            src_ref=src, dst_ref=dst, send_sem=send, recv_sem=recv,
            device_id=target, device_id_type=MESH,
        )

    z_copies = {
        offset: remote(
            z_in, near_z.at[2 - offset], z_send.at[2 + offset], z_recv.at[2 - offset],
            device(me + offset),
        )
        for offset in offsets
    }
    for offset in offsets:
        @pl.when(present(me + offset))
        def _():
            z_copies[offset].start()
    far_copies, part_copies, back_copies, side_copies = [], [], [], []
    for k in range(CHUNKS):
        piece = dosage.at[:, pl.ds(k * width, width)]
        far_copies.append(
            remote(piece, far_raw.at[k], far_send.at[k], far_recv.at[k], device(onward))
        )
        part_copies.append(
            remote(piece, part_raw.at[k], part_send.at[k], part_recv.at[k], device(partner))
        )
        back_copies.append(
            remote(back_out.at[k], back_in.at[k], back_send.at[k], back_recv.at[k], device(source))
        )
        side_copies.append(
            remote(side_out.at[k], side_in.at[k], side_send.at[k], side_recv.at[k], device(partner))
        )
    for k in range(CHUNKS):
        @pl.when(has_onward)
        def _():
            far_copies[k].start()
        part_copies[k].start()

    def gram(left, right):
        product = lax.dot_general(
            left, right, (((0,), (0,)), ((), ())), preferred_element_type=jnp.float32
        )
        return product * (1.0 / samples)

    def keep(flag, tile):
        return jnp.where(flag > 0, tile, jnp.zeros_like(tile)).astype(jnp.bfloat16)

    def span(k):
        return pl.ds(k * width, width)

    def columns(offset, k):
        start = (BAND + offset) * block + k * width
        return pl.ds(pl.multiple_of(start, 128), width)

    def weigh(tile, scores):
        return lax.dot_general(
            scores, tile, (((1,), (1,)), ((), ())), preferred_element_type=jnp.float32
        )

    def tile_at(offset):
        start = (BAND + offset) * block
        return out[:, pl.ds(pl.multiple_of(start, 128), block)]

    flag_far, flag_part, flag_side = flags[0], flags[1], flags[2]
    flag_pair = flags[3]
    flag_back = flags[4]
    own_z = z_in[...]

    for k in range(CHUNKS):
        loads[k].wait()
        own[k] = standardize(raw[k])
    for a in range(CHUNKS):
        for b in range(CHUNKS):
            out[span(a), columns(0, b)] = gram(own[a], own[b]).astype(jnp.bfloat16)
    smoothed = weigh(tile_at(0), own_z)

    for k in range(CHUNKS):
        @pl.when(has_source)
        def _():
            far_copies[k].wait_recv()
        far[k] = standardize(far_raw[k])
        for a in range(CHUNKS):
            back_out[k, :, span(a)] = gram(far[k], own[a]).astype(jnp.bfloat16)
        for a in range(CHUNKS):
            out[span(a), columns(2 * sign, k)] = keep(flag_far, gram(own[a], far[k]))
        @pl.when(has_source)
        def _():
            back_copies[k].start()
        part_copies[k].wait_recv()
        part[k] = standardize(part_raw[k])
        if k < CHUNKS - 1:
            for a in range(CHUNKS):
                out[span(a), columns(sign, k)] = keep(flag_part, gram(own[a], part[k]))
    for k in range(CHUNKS):
        for a in range(CHUNKS):
            side_out[k, span(a), :] = gram(part[a], far[k]).astype(jnp.bfloat16)
        @pl.when(has_source)
        def _():
            side_copies[k].start()
    for a in range(CHUNKS):
        out[span(a), columns(sign, CHUNKS - 1)] = keep(
            flag_part, gram(own[a], part[CHUNKS - 1])
        )

    for offset in offsets:
        @pl.when(present(me + offset))
        def _():
            z_copies[offset].wait_send()
    for offset in offsets:
        @pl.when(present(me - offset))
        def _():
            z_copies[offset].wait_recv()
    far_z, part_z = near_z[BAND + 2 * sign], near_z[BAND + sign]
    part_term = weigh(tile_at(sign), part_z)
    far_term = weigh(tile_at(2 * sign), far_z)
    form = (smoothed + part_term + 2.0 * far_term) * own_z.astype(jnp.float32)
    smoothed = smoothed + part_term + far_term
    pair_term = jnp.zeros_like(smoothed)
    for k in range(CHUNKS):
        tile = side_out[k]
        pair_term = pair_term + weigh(keep(flag_pair, tile), far_z[:, k * width : (k + 1) * width])
    form = form + pair_term * part_z.astype(jnp.float32)
    sum_out[0] = jnp.broadcast_to(jnp.sum(form[0:1], axis=1, keepdims=True), (8, 128))

    col_copies = [
        remote(sum_out.at[0], col_sums.at[i], col_send.at[i], col_recv.at[i], (row, (col + i) % cols))
        for i in range(1, cols)
    ]
    for copy in col_copies:
        copy.start()
    total = sum_out[0]
    for i in range(1, cols):
        col_copies[i - 1].wait()
        total = total + col_sums[i]
    sum_out[1] = total
    row_copies = [
        remote(sum_out.at[1], row_sums.at[i], row_send.at[i], row_recv.at[i], ((row + i) % rows, col))
        for i in range(1, rows)
    ]
    for copy in row_copies:
        copy.start()

    back_z, side_z = near_z[BAND - 2 * sign], near_z[BAND - sign]
    for k in range(CHUNKS):
        @pl.when(has_onward)
        def _():
            back_copies[k].wait_recv()
        start = pl.multiple_of((BAND - 2 * sign) * block, 128)
        out[span(k), pl.ds(start, block)] = keep(flag_back, back_in[k])
    smoothed = smoothed + weigh(tile_at(-2 * sign), back_z)
    for i in range(1, rows):
        row_copies[i - 1].wait()
        total = total + row_sums[i]
    quad[...] = total
    for k in range(CHUNKS):
        @pl.when(has_onward)
        def _():
            side_copies[k].wait_recv()
        out[:, columns(-sign, k)] = keep(flag_side, side_in[k])
    smoothed = smoothed + weigh(tile_at(-sign), side_z)
    smooth[...] = smoothed
    for k in range(CHUNKS):
        @pl.when(has_onward)
        def _():
            far_copies[k].wait_send()
        part_copies[k].wait_send()
        @pl.when(has_source)
        def _():
            back_copies[k].wait_send()
            side_copies[k].wait_send()


def body(rows, cols, dosage, zscores, band_reach):
    samples, block = dosage.shape
    count = rows * cols
    position = lax.axis_index(AXES)
    sign = 1 - 2 * (position % 2)
    width = block // CHUNKS

    def allowed(first, second):
        inside = (first >= 0) & (first < count) & (second >= 0) & (second < count)
        reach = jnp.minimum(
            band_reach[jnp.clip(first, 0, count - 1)], band_reach[jnp.clip(second, 0, count - 1)]
        )
        return (inside & (jnp.abs(first - second) <= reach)).astype(jnp.int32)

    flags = jnp.stack([
        allowed(position, position + 2 * sign),
        allowed(position, position + sign),
        allowed(position, position - sign),
        allowed(position + sign, position + 2 * sign),
        allowed(position, position - 2 * sign),
    ])
    z_rows = jnp.broadcast_to(zscores[None], (ZROWS, block))
    chunked = pltpu.VMEM((CHUNKS, samples, width), jnp.bfloat16)
    vmem = pl.BlockSpec(memory_space=pltpu.VMEM)
    dma = pltpu.SemaphoreType.DMA
    out, smooth, quad = pl.pallas_call(
        functools.partial(kernel, rows, cols),
        out_shape=(
            jax.ShapeDtypeStruct((block, (2 * BAND + 1) * block), jnp.bfloat16),
            jax.ShapeDtypeStruct((ZROWS, block), jnp.float32),
            jax.ShapeDtypeStruct((8, 128), jnp.float32),
        ),
        in_specs=[
            pl.BlockSpec(memory_space=pltpu.SMEM),
            pl.BlockSpec(memory_space=pl.ANY),
            vmem,
        ],
        out_specs=(vmem, vmem, vmem),
        scratch_shapes=[
            chunked, chunked, chunked, chunked, chunked, chunked,
            pltpu.VMEM((CHUNKS, width, block), jnp.bfloat16),
            pltpu.VMEM((CHUNKS, block, width), jnp.bfloat16),
            pltpu.VMEM((CHUNKS, width, block), jnp.bfloat16),
            pltpu.VMEM((CHUNKS, block, width), jnp.bfloat16),
            pltpu.VMEM((2 * BAND + 1, ZROWS, block), jnp.bfloat16),
            pltpu.VMEM((cols, 8, 128), jnp.float32),
            pltpu.VMEM((rows, 8, 128), jnp.float32),
            pltpu.VMEM((2, 8, 128), jnp.float32),
            dma((CHUNKS,)),
            dma((CHUNKS,)), dma((CHUNKS,)), dma((CHUNKS,)), dma((CHUNKS,)),
            dma((CHUNKS,)), dma((CHUNKS,)), dma((CHUNKS,)), dma((CHUNKS,)),
            dma((2 * BAND + 1,)), dma((2 * BAND + 1,)),
            dma((cols,)), dma((cols,)), dma((rows,)), dma((rows,)),
        ],
        compiler_params=pltpu.CompilerParams(
            collective_id=0, has_side_effects=True, vmem_limit_bytes=60 * 1024 * 1024
        ),
    )(flags, dosage, z_rows)
    quadratic = quad[0, 0] / (count * block)
    return (out, smooth[0], quadratic)


def solution(mesh):
    placed = (P(None, AXES), P(AXES), P())
    rows, cols = (mesh.shape[name] for name in AXES)
    return jax.shard_map(
        functools.partial(body, rows, cols),
        mesh=mesh,
        in_specs=placed,
        out_specs=(P(AXES, None), P(AXES), P()),
        check_vma=False,
    )
```

time: 226 us -> 117 us (0.52)
  Pallas kernels: 0 us -> 95.9 us
  waiting for transfers between devices: 88 us -> 0 us
  starting transfers between devices: 43.9 us -> 0 us
  blocking collectives: 42 us -> 0 us
  matrix products: 17.5 us -> 0 us
  local copies, waits for them, and re-layouts: 19.9 us -> 11.1 us
  other arithmetic: 6.11 us -> 0.52 us
  between operations: 6.25 us -> 9.1 us
    pallas_call x0 -> x1, Pallas kernels: none -> 95.9 us  [body(): pl.pallas_call(functools.partial(kernel, rows, cols), out_shape=(jax.Shap...]
    ppermute x8 -> x0, waiting for transfers between devices: 88 us -> none  [passed_along(): lax.ppermute(value, axis, [(source, source + steps) for source in range(i...]
    ppermute x8 -> x0, starting transfers between devices: 43.9 us -> none  [passed_along(): lax.ppermute(value, axis, [(source, source + steps) for source in range(i...]
    psum x1 -> x0, blocking collectives: 42 us -> none  [body(): total = lax.psum(jnp.sum(own_z * smoothed), ('row', 'col'))]
    dot_general x8 -> x0, matrix products: 17.5 us -> none  [the longest x3 14.7 us: make_tile(): lax.dot_general(left, right, (((0,), (0,)), ((), ())), preferred_element_...]
    unnamed x19 -> x1, local copies, waits for them, and re-layouts: 13.3 us -> 5.62 us
    reduce_sum x3 -> x0, other arithmetic: 4.09 us -> none  [the longest x1 2.22 us: standardize(): column_mean = jnp.mean(values, axis=0)]
    slice x0 -> x2, local copies, waits for them, and re-layouts: none -> 2.53 us  [the longest x1 1.34 us: body(): return (out, smooth[0], quadratic)]
  transfers between devices with their start and end apart: 8 -> 0, of which waited for: 3 -> 0; matrix products, arithmetic and copies ran while one was open for 7% -> 0% of each run, Pallas kernels for 0% -> 0%
where the time goes in v1:
time: 117 us
  Pallas kernels  95.9 us (82%)
  local copies, waits for them, and re-layouts  11.1 us (9%)
  between operations  9.1 us (8%)
    pallas_call x1, Pallas kernels, body(): pl.pallas_call(functools.partial(kernel, rows, cols), out_shape=(jax.Shap...  95.9 us
    unnamed x1, local copies, waits for them, and re-layouts  5.62 us

profile of v1, /device:TPU:9, one launch (start us, length us, event | category | flops | bytes accessed | tf_op | source)
XLA Modules:
  0.0 116.6 jit_solution(16640098196893932979)
XLA Ops:
  0.7 1.5 %fusion = (s32[1]{0:T(128)}, s32[1]{0:T(128)}, s32[1]{0:T(128)}, s32[1]{0:T(128)}, s32[1]{0:T(128)}) fusion(s32[32]{0:T(128)} %param.5, s32[]{:T(128)S(6)} %min.63, s32[]{:T(128)S(6)} %min.55, s32[]{:T(128)S(6)} %min.52, s32[]{:T(128)S(6)} %min.51, s32[]{:T(128)S(6)} %min.58), kind=kLoop, calls=%fused_computation.1 | loop fusion | bytes 60 | tf_op jit(solution)/shard_map/dynamic_slice | solution.py:260
  8.8 0.1 stack.30
  8.9 0.5 stack.31.flags
  9.5 1.3 %broadcast_in_dim.2.z_in = bf16[16,768]{1,0:T(8,128)(2,1)} broadcast(bf16[768]{0:T(1024)(128)(2,1)} %param.4), dimensions={1} | broadcast | bytes 26112 | tf_op jit(solution)/shard_map/broadcast_in_dim | solution.py:271
  10.7 95.9 %shard_map.58 = (bf16[768,3840]{1,0:T(8,128)(2,1)}, f32[16,768]{1,0:T(8,128)}, f32[8,128]{1,0:T(8,128)}) custom-call(s32[5]{0:T(128)} %stack.31.flags, bf16[1536,768]{1,0:T(8,128)(2,1)} %dosage.1, bf16[16,768]{1,0:T(8,128)(2,1)} %broadcast_in_dim.2.z_in), custom_call_target="tpu_custom_call" | custom-call | tf_op jit(solution)/shard_map/pallas_call | solution.py:275
  106.6 1.2 %slice.7 = f32[1,1]{1,0:T(1,128)} slice(f32[8,128]{1,0:T(8,128)} %get-tuple-element.8), slice={[0:1], [0:1]} | slice | bytes 8 | tf_op jit(solution)/shard_map/slice | solution.py:308
  108.5 1.3 %slice_reduce_fusion = f32[768]{0:T(1024)} fusion(f32[16,768]{1,0:T(8,128)} %get-tuple-element.7), kind=kLoop, calls=%fused_computation | loop fusion | bytes 6144 | tf_op jit(solution)/shard_map/slice | solution.py:309
  109.8 5.6 %copy.7 = bf16[768,3840]{1,0:T(8,128)(2,1)} copy(bf16[768,3840]{1,0:T(8,128)(2,1)} %get-tuple-element.17) | data formatting | bytes 11796480

commit v2 on v1

--- a/solution.py
+++ b/solution.py
@@ -23,11 +23,11 @@
 
 
 def kernel(
-    rows, cols, flags, dosage, z_in, out, smooth, quad,
-    raw, far_raw, part_raw, own, far, part, back_out, side_out, back_in, side_in,
+    rows, cols, reach, dosage, z_in, result, smooth, quad,
+    out, raw, far_raw, part_raw, own, far, part, back_out, side_out, back_in, side_in,
     near_z, col_sums, row_sums, sum_out,
     local_sem, far_send, far_recv, part_send, part_recv, back_send, back_recv,
-    side_send, side_recv, z_send, z_recv, col_send, col_recv, row_send, row_recv,
+    side_send, side_recv, panel_sem, z_send, z_recv, col_send, col_recv, row_send, row_recv,
 ):
     samples, block = dosage.shape
     width = block // CHUNKS
@@ -54,6 +54,7 @@
         load.start()
         loads.append(load)
     near_z[...] = jnp.zeros_like(near_z)
+    near_z[BAND] = jnp.broadcast_to(z_in[...], near_z.shape[1:])
 
     barrier = pltpu.get_barrier_semaphore()
     peers = cols - 1 + rows - 1
@@ -83,7 +84,7 @@
 
     z_copies = {
         offset: remote(
-            z_in, near_z.at[2 - offset], z_send.at[2 + offset], z_recv.at[2 - offset],
+            near_z.at[BAND], near_z.at[2 - offset], z_send.at[2 + offset], z_recv.at[2 - offset],
             device(me + offset),
         )
         for offset in offsets
@@ -104,9 +105,13 @@
         back_copies.append(
             remote(back_out.at[k], back_in.at[k], back_send.at[k], back_recv.at[k], device(source))
         )
-        side_copies.append(
-            remote(side_out.at[k], side_in.at[k], side_send.at[k], side_recv.at[k], device(partner))
-        )
+        side_copies.append([
+            remote(
+                side_out.at[k, b], side_in.at[k, b], side_send.at[k, b], side_recv.at[k, b],
+                device(partner),
+            )
+            for b in range(CHUNKS)
+        ])
     for k in range(CHUNKS):
         @pl.when(has_onward)
         def _():
@@ -120,7 +125,7 @@
         return product * (1.0 / samples)
 
     def keep(flag, tile):
-        return jnp.where(flag > 0, tile, jnp.zeros_like(tile)).astype(jnp.bfloat16)
+        return jnp.where(flag, tile, jnp.zeros_like(tile)).astype(jnp.bfloat16)
 
     def span(k):
         return pl.ds(k * width, width)
@@ -138,10 +143,26 @@
         start = (BAND + offset) * block
         return out[:, pl.ds(pl.multiple_of(start, 128), block)]
 
-    flag_far, flag_part, flag_side = flags[0], flags[1], flags[2]
-    flag_pair = flags[3]
-    flag_back = flags[4]
-    own_z = z_in[...]
+    def allowed(first, second):
+        lowest = jnp.minimum(
+            reach[jnp.clip(first, 0, count - 1)], reach[jnp.clip(second, 0, count - 1)]
+        )
+        return present(first) & present(second) & (jnp.abs(first - second) <= lowest)
+
+    flag_far, flag_part = allowed(me, source), allowed(me, partner)
+    flag_back, flag_side = allowed(me, onward), allowed(me, me - sign)
+    flag_pair = allowed(partner, source)
+    own_z = near_z[BAND]
+    panels = []
+
+    def write_panel(offset):
+        start = pl.multiple_of((BAND + offset) * block, 128)
+        place = pl.ds(start, block)
+        panel = pltpu.make_async_copy(
+            out.at[:, place], result.at[:, place], panel_sem.at[len(panels)]
+        )
+        panel.start()
+        panels.append(panel)
 
     for k in range(CHUNKS):
         loads[k].wait()
@@ -150,6 +171,7 @@
         for b in range(CHUNKS):
             out[span(a), columns(0, b)] = gram(own[a], own[b]).astype(jnp.bfloat16)
     smoothed = weigh(tile_at(0), own_z)
+    write_panel(0)
 
     for k in range(CHUNKS):
         @pl.when(has_source)
@@ -158,26 +180,22 @@
         far[k] = standardize(far_raw[k])
         for a in range(CHUNKS):
             back_out[k, :, span(a)] = gram(far[k], own[a]).astype(jnp.bfloat16)
-        for a in range(CHUNKS):
-            out[span(a), columns(2 * sign, k)] = keep(flag_far, gram(own[a], far[k]))
         @pl.when(has_source)
         def _():
             back_copies[k].start()
         part_copies[k].wait_recv()
         part[k] = standardize(part_raw[k])
-        if k < CHUNKS - 1:
-            for a in range(CHUNKS):
-                out[span(a), columns(sign, k)] = keep(flag_part, gram(own[a], part[k]))
-    for k in range(CHUNKS):
+        blocks = [(a, k) for a in range(k + 1)] + [(k, b) for b in range(k)]
+        for a, b in blocks:
+            side_out[a, b] = gram(part[a], far[b]).astype(jnp.bfloat16)
+            @pl.when(has_source)
+            def _():
+                side_copies[a][b].start()
         for a in range(CHUNKS):
-            side_out[k, span(a), :] = gram(part[a], far[k]).astype(jnp.bfloat16)
-        @pl.when(has_source)
-        def _():
-            side_copies[k].start()
-    for a in range(CHUNKS):
-        out[span(a), columns(sign, CHUNKS - 1)] = keep(
-            flag_part, gram(own[a], part[CHUNKS - 1])
-        )
+            out[span(a), columns(2 * sign, k)] = keep(flag_far, gram(own[a], far[k]))
+            out[span(a), columns(sign, k)] = keep(flag_part, gram(own[a], part[k]))
+    write_panel(2 * sign)
+    write_panel(sign)
 
     for offset in offsets:
         @pl.when(present(me + offset))
@@ -192,12 +210,15 @@
     far_term = weigh(tile_at(2 * sign), far_z)
     form = (smoothed + part_term + 2.0 * far_term) * own_z.astype(jnp.float32)
     smoothed = smoothed + part_term + far_term
-    pair_term = jnp.zeros_like(smoothed)
-    for k in range(CHUNKS):
-        tile = side_out[k]
-        pair_term = pair_term + weigh(keep(flag_pair, tile), far_z[:, k * width : (k + 1) * width])
-    form = form + pair_term * part_z.astype(jnp.float32)
-    sum_out[0] = jnp.broadcast_to(jnp.sum(form[0:1], axis=1, keepdims=True), (8, 128))
+    form_sum = jnp.sum(form[0:1], axis=1, keepdims=True)
+    for a in range(CHUNKS):
+        pair_term = jnp.zeros((ZROWS, width), jnp.float32)
+        for b in range(CHUNKS):
+            scores = far_z[:, b * width : (b + 1) * width]
+            pair_term = pair_term + weigh(keep(flag_pair, side_out[a, b]), scores)
+        pair_term = pair_term * part_z[:, a * width : (a + 1) * width].astype(jnp.float32)
+        form_sum = form_sum + jnp.sum(pair_term[0:1], axis=1, keepdims=True)
+    sum_out[0] = jnp.broadcast_to(form_sum, (8, 128))
 
     col_copies = [
         remote(sum_out.at[0], col_sums.at[i], col_send.at[i], col_recv.at[i], (row, (col + i) % cols))
@@ -224,18 +245,21 @@
             back_copies[k].wait_recv()
         start = pl.multiple_of((BAND - 2 * sign) * block, 128)
         out[span(k), pl.ds(start, block)] = keep(flag_back, back_in[k])
+    write_panel(-2 * sign)
     smoothed = smoothed + weigh(tile_at(-2 * sign), back_z)
     for i in range(1, rows):
         row_copies[i - 1].wait()
         total = total + row_sums[i]
-    quad[...] = total
-    for k in range(CHUNKS):
-        @pl.when(has_onward)
-        def _():
-            side_copies[k].wait_recv()
-        out[:, columns(-sign, k)] = keep(flag_side, side_in[k])
+    quad[...] = total[0:1, 0:1] / (count * block)
+    for k in range(CHUNKS):
+        for a, b in [(a, k) for a in range(k + 1)] + [(k, b) for b in range(k)]:
+            @pl.when(has_onward)
+            def _():
+                side_copies[a][b].wait_recv()
+            out[span(a), columns(-sign, b)] = keep(flag_side, side_in[a, b])
+    write_panel(-sign)
     smoothed = smoothed + weigh(tile_at(-sign), side_z)
-    smooth[...] = smoothed
+    smooth[...] = smoothed[0:1]
     for k in range(CHUNKS):
         @pl.when(has_onward)
         def _():
@@ -244,31 +268,15 @@
         @pl.when(has_source)
         def _():
             back_copies[k].wait_send()
-            side_copies[k].wait_send()
+            for b in range(CHUNKS):
+                side_copies[k][b].wait_send()
+    for panel in panels:
+        panel.wait()
 
 
 def body(rows, cols, dosage, zscores, band_reach):
     samples, block = dosage.shape
-    count = rows * cols
-    position = lax.axis_index(AXES)
-    sign = 1 - 2 * (position % 2)
     width = block // CHUNKS
-
-    def allowed(first, second):
-        inside = (first >= 0) & (first < count) & (second >= 0) & (second < count)
-        reach = jnp.minimum(
-            band_reach[jnp.clip(first, 0, count - 1)], band_reach[jnp.clip(second, 0, count - 1)]
-        )
-        return (inside & (jnp.abs(first - second) <= reach)).astype(jnp.int32)
-
-    flags = jnp.stack([
-        allowed(position, position + 2 * sign),
-        allowed(position, position + sign),
-        allowed(position, position - sign),
-        allowed(position + sign, position + 2 * sign),
-        allowed(position, position - 2 * sign),
-    ])
-    z_rows = jnp.broadcast_to(zscores[None], (ZROWS, block))
     chunked = pltpu.VMEM((CHUNKS, samples, width), jnp.bfloat16)
     vmem = pl.BlockSpec(memory_space=pltpu.VMEM)
     dma = pltpu.SemaphoreType.DMA
@@ -276,37 +284,38 @@
         functools.partial(kernel, rows, cols),
         out_shape=(
             jax.ShapeDtypeStruct((block, (2 * BAND + 1) * block), jnp.bfloat16),
-            jax.ShapeDtypeStruct((ZROWS, block), jnp.float32),
-            jax.ShapeDtypeStruct((8, 128), jnp.float32),
+            jax.ShapeDtypeStruct((1, block), jnp.float32),
+            jax.ShapeDtypeStruct((1, 1), jnp.float32),
         ),
         in_specs=[
             pl.BlockSpec(memory_space=pltpu.SMEM),
             pl.BlockSpec(memory_space=pl.ANY),
             vmem,
         ],
-        out_specs=(vmem, vmem, vmem),
+        out_specs=(pl.BlockSpec(memory_space=pl.ANY), vmem, vmem),
         scratch_shapes=[
+            pltpu.VMEM((block, (2 * BAND + 1) * block), jnp.bfloat16),
             chunked, chunked, chunked, chunked, chunked, chunked,
             pltpu.VMEM((CHUNKS, width, block), jnp.bfloat16),
-            pltpu.VMEM((CHUNKS, block, width), jnp.bfloat16),
+            pltpu.VMEM((CHUNKS, CHUNKS, width, width), jnp.bfloat16),
             pltpu.VMEM((CHUNKS, width, block), jnp.bfloat16),
-            pltpu.VMEM((CHUNKS, block, width), jnp.bfloat16),
+            pltpu.VMEM((CHUNKS, CHUNKS, width, width), jnp.bfloat16),
             pltpu.VMEM((2 * BAND + 1, ZROWS, block), jnp.bfloat16),
             pltpu.VMEM((cols, 8, 128), jnp.float32),
             pltpu.VMEM((rows, 8, 128), jnp.float32),
             pltpu.VMEM((2, 8, 128), jnp.float32),
             dma((CHUNKS,)),
             dma((CHUNKS,)), dma((CHUNKS,)), dma((CHUNKS,)), dma((CHUNKS,)),
-            dma((CHUNKS,)), dma((CHUNKS,)), dma((CHUNKS,)), dma((CHUNKS,)),
+            dma((CHUNKS,)), dma((CHUNKS,)), dma((CHUNKS, CHUNKS)), dma((CHUNKS, CHUNKS)),
+            dma((2 * BAND + 1,)),
             dma((2 * BAND + 1,)), dma((2 * BAND + 1,)),
             dma((cols,)), dma((cols,)), dma((rows,)), dma((rows,)),
         ],
         compiler_params=pltpu.CompilerParams(
             collective_id=0, has_side_effects=True, vmem_limit_bytes=60 * 1024 * 1024
         ),
-    )(flags, dosage, z_rows)
-    quadratic = quad[0, 0] / (count * block)
-    return (out, smooth[0], quadratic)
+    )(band_reach, dosage, zscores.reshape(1, block))
+    return (out, smooth.reshape(block), quad.reshape(()))
 
 
 def solution(mesh):

time: 117 us -> 102 us (0.87)
  between operations: 9.1 us -> 2.34 us
  Pallas kernels: 95.9 us -> 90.7 us
  local copies, waits for them, and re-layouts: 11.1 us -> 6.89 us
    pallas_call x1, Pallas kernels: 95.9 us -> 90.7 us  [body(): pl.pallas_call(functools.partial(kernel, rows, cols), out_shape=(jax.Shap...]
    slice x2 -> x0, local copies, waits for them, and re-layouts: 2.53 us -> none  [the longest x1 1.34 us: body(): return (out, smooth[0], quadratic)]
    dynamic_slice x1 -> x0, local copies, waits for them, and re-layouts: 1.52 us -> none  [allowed(): band_reach[jnp.clip(second, 0, count - 1)]]
    broadcast_in_dim x1 -> x0, local copies, waits for them, and re-layouts: 1.29 us -> none  [body(): z_rows = jnp.broadcast_to(zscores[None], (ZROWS, block))]
    pallas_call x0 -> x1, other arithmetic: none -> 1.28 us  [body(): pl.pallas_call(functools.partial(kernel, rows, cols), out_shape=(jax.Shap...]
    reshape x0 -> x1, local copies, waits for them, and re-layouts: none -> 1.26 us  [body(): zscores.reshape(1, block)]
where the time goes in v2:
time: 102 us; the launch traced here: 101 us
  Pallas kernels  90.7 us (89%)
  local copies, waits for them, and re-layouts  6.89 us (7%)
  between operations  2.34 us (2%)
  other arithmetic  1.28 us (1%)
    pallas_call x1, Pallas kernels, body(): pl.pallas_call(functools.partial(kernel, rows, cols), out_shape=(jax.Shap...  90.7 us
    unnamed x1, local copies, waits for them, and re-layouts  5.62 us

profile of v2, /device:TPU:9, one launch (start us, length us, event | category | flops | bytes accessed | tf_op | source)
XLA Modules:
  0.0 101.2 jit_solution(9197137455204756277)
XLA Ops:
  0.6 1.3 %reshape.15.z_in = bf16[1,768]{1,0:T(2,128)(2,1)} reshape(bf16[768]{0:T(1024)(128)(2,1)} %param.4) | data formatting | bytes 3072 | tf_op jit(solution)/shard_map/reshape | solution.py:317
  1.9 90.7 %shard_map.58 = (bf16[768,3840]{1,0:T(8,128)(2,1)}, f32[1,768]{1,0:T(1,128)}, f32[1,1]{1,0:T(1,128)}) custom-call(s32[32]{0:T(128)} %reach.1, bf16[1536,768]{1,0:T(8,128)(2,1)} %dosage.1, bf16[1,768]{1,0:T(2,128)(2,1)} %reshape.15.z_in), custom_call_target="tpu_custom_call" | custom-call | tf_op jit(solution)/shard_map/pallas_call | solution.py:283
  92.6 1.3 %reduce = f32[768]{0:T(1024)} reduce(f32[1,768]{1,0:T(1,128)} %get-tuple-element.7, f32[]{:T(128)} %constant), dimensions={0}, to_apply=%get-tuple-element.7.reduce_sub_computation | reduce | bytes 6148 | tf_op jit(solution)/shard_map/pallas_call | solution.py:283
  93.8 5.6 %copy.8 = bf16[768,3840]{1,0:T(8,128)(2,1)} copy(bf16[768,3840]{1,0:T(8,128)(2,1)} %get-tuple-element.12) | data formatting | bytes 11796480
